TPU v7x, 128 devices: a whole 4x4x4 slice. The times are simulated.
128 devices in a mesh: dp: 16 (over x, y), mp: 8 (over z, core).
Axes of the slice: x: 4, y: 4, z: 4, core: 2. Of those that a mesh axis runs over, the one named last changes fastest.
Arguments:
- activations: bfloat16 [16384, 4096], P(('dp', 'mp')), may hold values from -17 to 17
- output_grads: bfloat16 [16384, 14336], P('dp', 'mp'), may hold values from -0.046875 to 0.046875
- q_start: float32 [14336, 64], P('mp'), may hold values from -6 to 6
Outputs:
- new_error: bfloat16 [65536, 14336], P('dp', 'mp')
- q_factor: float32 [14336, 64], P('mp')
All inputs are finite; a program needn't handle non-finite values.
Results may differ from a plain program's by a relative error of at most 0.01.
Values may be sent and summed in bfloat16 or wider, within the bound.
A program may use at most 192 MiB of HBM per device.

v0:
```python
import jax
import jax.numpy as jnp
from jax import lax
from jax.sharding import PartitionSpec as P


def split_up(value, dim, count):
    before, after = (value.shape[:dim], value.shape[dim + 1 :])
    return jnp.moveaxis(value.reshape(*before, count, -1, *after), dim, 0)


def summed_on_arrival(value, axis, dim):
    count = lax.axis_size(axis)
    blocks = lax.all_to_all(split_up(value, dim, count), axis, 0, 0, tiled=True)
    return jnp.sum(blocks, axis=0)


def copy_for_each(value, axis):
    count = lax.axis_size(axis)
    return lax.all_to_all(
        jnp.broadcast_to(value[None], (count, *value.shape)), axis, 0, 0, tiled=True
    )


def taken_together(value, axis):
    return copy_for_each(value, axis).sum(axis=0)


def laid_out(blocks, dim):
    blocks = jnp.moveaxis(blocks, 0, dim)
    shape = blocks.shape
    return blocks.reshape(*shape[:dim], shape[dim] * shape[dim + 1], *shape[dim + 2 :])


def collect(value, axis, dim):
    return laid_out(copy_for_each(value, axis), dim)


def orthonormal(p_mean, gram_matrix):
    lower_tri = jnp.linalg.cholesky(gram_matrix)
    return lax.linalg.triangular_solve(
        lower_tri, p_mean, left_side=False, lower=True, transpose_a=True
    )


def split_parts(values):
    upper = values.astype(jnp.bfloat16)
    lower = (values - upper.astype(jnp.float32)).astype(jnp.bfloat16)
    return (upper, lower)


def per_device(activations, output_grads, q_start):
    contract_rows = (((0,), (0,)), ((), ()))
    replicas = lax.axis_size("dp")
    gathered = lax.all_gather(activations, "mp", axis=0, tiled=True)
    q_upper, q_lower = split_parts(q_start)
    projected = jnp.dot(output_grads, q_upper, preferred_element_type=jnp.float32)
    projected = projected + jnp.dot(output_grads, q_lower, preferred_element_type=jnp.float32)
    proj_upper, proj_lower = split_parts(projected)
    partial_p = lax.dot_general(
        gathered, proj_upper, contract_rows, preferred_element_type=jnp.float32
    )
    partial_p = partial_p + lax.dot_general(
        gathered, proj_lower, contract_rows, preferred_element_type=jnp.float32
    )
    gradient = lax.dot_general(
        gathered, output_grads, contract_rows, preferred_element_type=jnp.float32
    )
    row_block = summed_on_arrival(partial_p, "mp", 0)
    row_block = taken_together(row_block, "dp") / replicas
    block_gram = lax.dot_general(row_block, row_block, contract_rows)
    gram_matrix = taken_together(block_gram, "mp")
    ortho_rows = orthonormal(row_block, gram_matrix)
    p_ortho = collect(ortho_rows, "mp", 0)
    local_factor = lax.dot_general(gradient, p_ortho, contract_rows)
    q_factor = lax.psum(local_factor, "dp") / replicas
    decompressed = lax.dot_general(p_ortho, q_factor, (((1,), (1,)), ((), ())))
    new_error = (gradient - decompressed).astype(jnp.bfloat16)
    return (new_error, q_factor)


def solution(mesh):
    in_specs = (P(("dp", "mp"), None), P("dp", "mp"), P("mp", None))
    out_specs = (P("dp", "mp"), P("mp", None))
    return jax.shard_map(
        per_device, mesh=mesh, in_specs=in_specs, out_specs=out_specs, check_vma=False
    )
```

profile of v0, /device:TPU:1, one launch (start us, length us, event | category | flops | bytes accessed | tf_op | source)
XLA Modules:
  0.0 293.6 jit_solution(3268212242968762611)
XLA Ops:
  7.2 0.0 all-gather.2.cloned.1.call-start
  7.2 0.7 all-gather.2.cloned.1.call-update
  7.9 3.6 %convolution_bitcast_fusion = f32[1024,64]{0,1:T(8,128)S(1)} fusion(bf16[1024,1792]{1,0:T(8,128)(2,1)} %param.4, f32[1792,64]{0,1:T(8,128)} %param.5), kind=kOutput, calls=%fused_computation.3 | convolution fusion | flops 235339776 | bytes 4390912 | tf_op jit(solution)/shard_map/dot_general | solution.py:58
  11.5 3.3 %convolution_add_fusion.1 = f32[1024,64]{0,1:T(8,128)S(1)} fusion(f32[1024,64]{0,1:T(8,128)S(1)} %convolution_bitcast_fusion, bf16[1024,1792]{1,0:T(8,128)(2,1)} %param.4, f32[1792,64]{0,1:T(8,128)} %param.5), kind=kOutput, calls=%fused_computation.2 | convolution fusion | flops 235061248 | bytes 4653056 | tf_op jit(solution)/shard_map/dot_general | solution.py:57
  14.8 48.4 %all-gather.2.cloned.1.call-done = bf16[1024,4096]{1,0:T(8,128)(2,1)} async-done(((bf16[128,4096]{1,0:T(8,128)(2,1)}), bf16[1024,4096]{1,0:T(8,128)(2,1)}) %all-gather.2.cloned.1.call-update) | async-done | bytes 8388624 | tf_op jit(solution)/shard_map/all_gather | solution.py:55
  63.2 0.0 copy-start
  63.2 5.1 %fusion.9 = f32[64,4096]{1,0:T(8,128)S(1)} fusion(bf16[1024,4096]{1,0:T(8,128)(2,1)} %all-gather.2.cloned.1.call-done, f32[1024,64]{0,1:T(8,128)S(1)} %convolution_add_fusion.1), kind=kOutput, calls=%fused_computation.17 | convolution fusion | flops 536936448 | bytes 9699328 | tf_op jit(solution)/shard_map/dot_general | solution.py:60
  68.3 0.7 copy-done
  69.0 1.6 convolution_add_fusion
  70.6 0.1 copy.26
  70.6 18.2 %all_to_all.20 = f32[8,512,64]{1,2,0:T(8,128)S(1)} all-to-all(f32[8,512,64]{1,2,0:T(8,128)S(1)} %bitcast.31), channel_id=1, replica_groups=mesh['dp'=16,'mp'=8] {'mp'}, dimensions={0} | all-to-all | bytes 2097152 | tf_op jit(solution)/shard_map/all_to_all | solution.py:14
  88.8 0.1 reduce_sum.27
  88.9 0.3 broadcast_in_dim.7
  89.2 33.1 %all_to_all.21 = f32[16,512,64]{1,2,0:T(8,128)S(1)} all-to-all(f32[16,512,64]{1,2,0:T(8,128)S(1)} %broadcast_in_dim.7), channel_id=1, replica_groups=mesh['dp'=16,'mp'=8] {'dp'}, dimensions={0} | all-to-all | bytes 4194304 | tf_op jit(solution)/shard_map/all_to_all | solution.py:20
  122.2 0.2 reduce_sum.28
  122.4 0.1 fusion.2
  122.6 0.2 reshape.24
  122.8 10.2 %all_to_all.22 = f32[8,1,4096]{2,1,0:T(1,128)S(1)} all-to-all(f32[8,1,4096]{2,1,0:T(1,128)S(1)} %reshape.24), channel_id=1, replica_groups=mesh['dp'=16,'mp'=8] {'mp'}, dimensions={0} | all-to-all | bytes 262144 | tf_op jit(solution)/shard_map/all_to_all | solution.py:20
  132.9 0.5 broadcast.52
  133.5 1.0 reduce.6
  134.4 0.1 reshape.25
  134.6 0.1 copy.20
  134.6 5.8 %cholesky.16 = f32[64,64]{1,0:T(8,128)S(1)} custom-call(f32[64,64]{1,0:T(8,128)S(1)} %fusion.13), custom_call_target="Cholesky" | custom-call | tf_op jit(solution)/shard_map/jit(cholesky)/cholesky | solution.py:40
  140.5 0.6 compare_reduce_fusion
  141.2 0.7 fusion.11
  141.8 4.9 %custom-call.6 = f32[1,64,64]{1,2,0:T(8,128)S(1)} custom-call(f32[1,64,64]{2,1,0:T(8,128)S(1)} %fusion.11), custom_call_target="InvertDiagBlocksLowerTriangular" | custom-call | tf_op jit(solution)/shard_map/triangular_solve | solution.py:41
  146.7 0.3 fusion
  147.1 0.8 broadcast_in_dim.10
  147.9 4.3 %all-to-all-start.3 = ((bf16[8,512,64]{1,2,0:T(8,128)(2,1)}), bf16[8,512,64]{1,2,0:T(8,128)(2,1)S(1)}, u32[]{:S(2)}, u32[]{:S(2)}) async-start(bf16[8,512,64]{1,2,0:T(8,128)(2,1)} %broadcast_in_dim.10), calls=%async_computation.3 | async-start | bytes 1048576 | tf_op jit(solution)/shard_map/all_to_all | solution.py:20
  152.2 0.0 all-reduce.2.cloned.1.call-start
  152.2 22.9 %fusion.16 = f32[4096,1792]{1,0:T(8,128)} fusion(bf16[1024,4096]{1,0:T(8,128)(2,1)} %all-gather.2.cloned.1.call-done, bf16[1024,1792]{1,0:T(8,128)(2,1)} %param.4), kind=kOutput, calls=%fused_computation.30 | convolution fusion | flops 15032385536 | bytes 41418752 | tf_op jit(solution)/shard_map/dot_general | solution.py:66
  175.0 0.0 all-to-all-done.3
  175.1 12.8 %fusion.17 = f32[1792,64]{0,1:T(8,128)} fusion(f32[4096,1792]{1,0:T(8,128)} %fusion.16, bf16[4096,64]{0,1:T(8,128)(2,1)S(1)} %bitcast.28), kind=kOutput, calls=%fused_computation.31 | convolution fusion | flops 939524096 | bytes 30343168 | tf_op jit(solution)/shard_map/dot_general | solution.py:75
  187.8 0.0 all-reduce.2.cloned.1.call-update
  187.9 80.5 %all-reduce.2.cloned.1.call-done = f32[1792,64]{0,1:T(8,128)} async-done(((f32[1792,64]{0,1:T(8,128)}), f32[1792,64]{0,1:T(8,128)}) %all-reduce.2.cloned.1.call-update) | async-done | bytes 458768 | tf_op jit(solution)/shard_map/psum | solution.py:76
  268.4 1.0 broadcast_multiply_fusion
  269.4 0.0 copy-start.1
  269.4 17.3 %subtract_convert_fusion = bf16[4096,1792]{1,0:T(8,128)(2,1)} fusion(f32[4096,1792]{1,0:T(8,128)} %fusion.16, bf16[4096,64]{0,1:T(8,128)(2,1)S(1)} %bitcast.29, f32[1792,64]{0,1:T(8,128)S(1)} %broadcast_multiply_fusion), kind=kOutput, calls=%fused_computation | convolution fusion | flops 954204160 | bytes 45023232 | tf_op jit(solution)/shard_map/dot_general | solution.py:77
  286.7 0.0 copy-done.1
  (5 shorter events, 0.1 us)
Async XLA Ops:
  7.2 56.0 %all-gather.2.cloned.1.call-start = ((), (), s32[]{:S(2)}) async-start(), calls=%async_computation.4 | async-start | bytes 9437184 | tf_op jit(solution)/shard_map/all_gather | solution.py:55
  63.2 5.8 %copy-start = (bf16[1024,4096]{1,0:T(8,128)(2,1)S(1)}, bf16[1024,4096]{1,0:T(8,128)(2,1)}, u32[]{:S(2)}) copy-start(bf16[1024,4096]{1,0:T(8,128)(2,1)} %all-gather.2.cloned.1.call-done) | copy-start | bytes 25165828
  147.9 27.1 %all-to-all-start.3 = ((bf16[8,512,64]{1,2,0:T(8,128)(2,1)}), bf16[8,512,64]{1,2,0:T(8,128)(2,1)S(1)}, u32[]{:S(2)}, u32[]{:S(2)}) async-start(bf16[8,512,64]{1,2,0:T(8,128)(2,1)} %broadcast_in_dim.10), calls=%async_computation.3 | async-start | bytes 1048576 | tf_op jit(solution)/shard_map/all_to_all | solution.py:20
  152.2 116.2 %all-reduce.2.cloned.1.call-start = ((), (), s32[]{:S(2)}) async-start(), calls=%async_computation.5 | async-start | bytes 917504 | tf_op jit(solution)/shard_map/psum | solution.py:76
  269.4 17.3 %copy-start.1 = (f32[1792,64]{0,1:T(8,128)}, f32[1792,64]{0,1:T(8,128)S(1)}, u32[]{:S(2)}) copy-start(f32[1792,64]{0,1:T(8,128)S(1)} %broadcast_multiply_fusion) | copy-start | bytes 1376260
Sparse Core Ops, SparseCore 0:
  9.7 53.4 all-gather.1
  188.0 80.3 all-reduce.1
where the time goes:
time: 295 us; the launch traced here: 294 us
  waiting for transfers between devices  130 us (44%)
  matrix products  67 us (23%)
  blocking collectives  61.4 us (21%)
  other arithmetic  14.3 us (5%)
  between operations  14.2 us (5%)
  starting transfers between devices  4.3 us (1%)
    psum x1, waiting for transfers between devices, per_device(): q_factor = lax.psum(local_factor, 'dp') / replicas  80.5 us
    all_gather x1, waiting for transfers between devices, per_device(): gathered = lax.all_gather(activations, 'mp', axis=0, tiled=True)  48.4 us
    all_to_all x2, blocking collectives, copy_for_each(): lax.all_to_all(jnp.broadcast_to(value[None], (count, *value.shape)), axis...  43.2 us
    dot_general x1, matrix products, per_device(): lax.dot_general(gathered, output_grads, contract_rows, preferred_element_...  22.9 us
    all_to_all x1, blocking collectives, summed_on_arrival(): blocks = lax.all_to_all(split_up(value, dim, count), axis, 0, 0, tiled=True)  18.2 us
    dot_general x1, matrix products, per_device(): decompressed = lax.dot_general(p_ortho, q_factor, (((1,), (1,)), ((), ())))  17.3 us
    dot_general x1, matrix products, per_device(): local_factor = lax.dot_general(gradient, p_ortho, contract_rows)  12.8 us
    another operation x3, other arithmetic, orthonormal(): lower_tri = jnp.linalg.cholesky(gram_matrix)  6.52 us
  transfers between devices with their start and end apart: 3, of which 2 were waited for; matrix products, arithmetic and copies ran while one was open for 10% of the time, Pallas kernels for 0%

commit v1 on v0

v1 whole, which is shorter than its diff:
```python
import jax
import jax.numpy as jnp
from jax import lax
from jax.experimental import pallas as pl
from jax.experimental.pallas import tpu as pltpu
from jax.sharding import PartitionSpec as P

MESH = pl.DeviceIdType.MESH
BF, F32 = jnp.bfloat16, jnp.float32
D, FFL, R, TOK = 4096, 1792, 64, 1024
BLK, NB = 128, 32
CB = 14
ROWS = 1024
NN = (((1,), (0,)), ((), ()))
NT = (((1,), (1,)), ((), ()))
TN = (((0,), (0,)), ((), ()))


def dot(a, b, dims=NN):
    return lax.dot_general(a, b, dims, preferred_element_type=F32)


def halves(v):
    upper = v.astype(BF)
    return upper, (v - upper.astype(F32)).astype(BF)


def dot3(a, b, dims=NN):
    (ah, al), (bh, bl) = halves(a), halves(b)
    return dot(ah, bh, dims) + (dot(ah, bl, dims) + dot(al, bh, dims))


def factor_kernel(
    x_hbm, y_hbm, q_hbm, g0, g1, g2, g3, p_out, q_out, c_out,
    x_v, y_v, q_v, xt, af, a_s, a_r, pown, pc_s, pc_r, px_s, px_r, py_f, py_s, py_r, pz, pt,
    xpb, qf, qs, qx_r, qy_f, qy_s, qy_r, qa, linv,
    ld_sem, a_ss, a_rs, c_ss, c_rs, x_ss, x_rs, y_ss, y_rs, z_ss, z_rs,
    gy_ss, gy_rs, gx_ss, gx_rs, gc_ss, gc_rs, xp_ss, xp_rs,
    qx_ss, qx_rs, qy_ss, qy_rs, hy_ss, hy_rs, hx_ss, hx_rs,
    own_s, own_r, up_s, up_r, dn_s, dn_r, fw_s, fw_r, pf_s, pf_r,
):
    g_refs = (g0, g1, g2, g3)
    r, m = lax.axis_index("dp"), lax.axis_index("mp")
    x, y = r // 4, lax.rem(r, 4)
    z, c = m // 2, lax.rem(m, 2)
    partner = {"dp": r, "mp": z * 2 + (1 - c)}

    def mp_peer(k):
        return {"dp": r, "mp": lax.rem(m + k, 8)}

    def x_peer(k):
        return {"dp": lax.rem(x + k, 4) * 4 + y, "mp": m}

    def y_peer(k):
        return {"dp": x * 4 + lax.rem(y + k, 4), "mp": m}

    def z_peer(k):
        return {"dp": r, "mp": lax.rem(z + k, 4) * 2 + c}

    sent = []

    def push(src, dst, ssem, rsem, dev):
        cp = pltpu.make_async_remote_copy(
            src_ref=src, dst_ref=dst, send_sem=ssem, recv_sem=rsem, device_id=dev, device_id_type=MESH
        )
        cp.start()
        sent.append(cp)
        return cp

    x_cp = pltpu.make_async_copy(x_hbm, x_v, ld_sem.at[0])
    q_cp = pltpu.make_async_copy(q_hbm, q_v, ld_sem.at[1])
    y_cps = [
        pltpu.make_async_copy(y_hbm.at[pl.ds(256 * i, 256)], y_v.at[pl.ds(256 * i, 256)], ld_sem.at[2 + i])
        for i in range(4)
    ]
    x_cp.start()
    q_cp.start()
    for cp in y_cps:
        cp.start()

    bar = pltpu.get_barrier_semaphore()
    for dev in [mp_peer(k) for k in range(1, 8)] + [f(k) for f in (x_peer, y_peer) for k in (1, 2, 3)]:
        pl.semaphore_signal(bar, inc=1, device_id=dev, device_id_type=MESH)

    x_cp.wait()
    for i in range(4):
        xt[m, 1024 * i : 1024 * (i + 1), :] = x_v[:, 1024 * i : 1024 * (i + 1)].T

    pl.semaphore_wait(bar, 13)
    own = push(xt.at[m], xt.at[m], own_s.at[0], own_r.at[0], partner)

    q_cp.wait()
    qh, ql = halves(q_v[...])
    qq = jnp.concatenate([qh, ql], axis=0)
    for i in range(4):
        y_cps[i].wait()
        both = dot(qq, y_v[256 * i : 256 * (i + 1), :], NT)
        at = both[:R] + both[R:]
        for h in range(2):
            blk = at[:, BLK * h : BLK * (h + 1)]
            af[2 * i + h] = blk
            a_s[2 * i + h] = blk.astype(BF)
    a_cps = []
    for k in range(1, 8):
        to = lax.rem(m + k, 8)
        a_cps.append(push(a_s.at[to], a_r.at[k - 1], a_ss.at[k - 1], a_rs.at[k - 1], mp_peer(k)))

    def rows(j):
        return pl.ds(ROWS * j, ROWS)

    def ring_own(j_up, j_dn):
        u = push(xt.at[m, rows(j_up)], xt.at[m, rows(j_up)], up_s.at[j_up], up_r.at[j_up], z_peer(1))
        d = push(xt.at[m, rows(j_dn)], xt.at[m, rows(j_dn)], dn_s.at[j_dn], dn_r.at[j_dn], z_peer(3))
        return {("u", j_up): u, ("d", j_dn): d}

    ring = {}
    ring.update(ring_own(0, 2))
    ring.update(ring_own(1, 3))

    def g_tile(zz, j, first):
        def body(h, carry):
            at_row = pl.multiple_of(512 * h, 512)
            src = pl.multiple_of(ROWS * j + 512 * h, 512)
            lhs = jnp.concatenate([xt[2 * zz, pl.ds(src, 512), :], xt[2 * zz + 1, pl.ds(src, 512), :]], axis=1)
            for n in range(7):
                w = y_v[pl.ds(pl.multiple_of(256 * zz, 256), 256), 256 * n : 256 * (n + 1)]
                prod = dot(lhs, w)
                spot = (pl.ds(at_row, 512), slice(256 * n, 256 * (n + 1)))
                if first:
                    g_refs[j][spot] = prod
                else:
                    g_refs[j][spot] = g_refs[j][spot] + prod
            return carry

        lax.fori_loop(0, 2, body, 0)

    own.wait_recv()
    for j in range(4):
        g_tile(z, j, True)

    at = af[m]
    for k in range(1, 8):
        a_cps[k - 1].wait_recv()
    for k in range(1, 8):
        at = at + a_r[k - 1].astype(F32)

    ath, atl = halves(at)
    aa = jnp.concatenate([ath, atl], axis=0)

    def p_part(half, write):
        for b in range(8):
            col = pl.multiple_of(half * 2048 + 256 * b, 256)
            both = dot(aa, x_v[:, pl.ds(col, 256)])
            s = both[:R] + both[R:]
            write(2 * b, s[:, :BLK])
            write(2 * b + 1, s[:, BLK:])

    def put_send(b, v):
        pc_s[b] = v.astype(BF)

    def put_own(b, v):
        pown[b] = v

    p_part(1 - c, put_send)
    pc = push(pc_s, pc_r, c_ss.at[0], c_rs.at[0], partner)
    p_part(c, put_own)
    pc.wait_recv()
    tot = pown[...] + pc_r[...].astype(F32)
    pown[...] = tot
    px_s[...] = tot.astype(BF)
    cps = []
    for k in (1, 2, 3):
        to = lax.rem(x + k, 4)
        cps.append(push(px_s.at[pl.ds(4 * to, 4)], px_r.at[k - 1], x_ss.at[k - 1], x_rs.at[k - 1], x_peer(k)))
    tot = pown[pl.ds(4 * x, 4)]
    for k in (1, 2, 3):
        cps[k - 1].wait_recv()
        tot = tot + px_r[k - 1].astype(F32)
    py_f[...] = tot
    py_s[...] = tot.astype(BF)
    cps = []
    for k in (1, 2, 3):
        to = lax.rem(y + k, 4)
        cps.append(push(py_s.at[to], py_r.at[k - 1], y_ss.at[k - 1], y_rs.at[k - 1], y_peer(k)))
    tot = py_f[y]
    for k in (1, 2, 3):
        cps[k - 1].wait_recv()
        tot = tot + py_r[k - 1].astype(F32)
    pz[z] = tot * (1.0 / 16.0)
    cps = [push(pz.at[z], pz.at[z], z_ss.at[k - 1], z_rs.at[k - 1], z_peer(k)) for k in (1, 2, 3)]
    ring.update(ring_own(2, 0))
    ring.update(ring_own(3, 1))
    for cp in cps:
        cp.wait_recv()
    blk = c * 16 + x * 4 + y
    pt[blk] = ((pz[0] + pz[1]) + (pz[2] + pz[3])).astype(BF)

    cps = [push(pt.at[blk], pt.at[blk], gy_ss.at[k - 1], gy_rs.at[k - 1], y_peer(k)) for k in (1, 2, 3)]
    for cp in cps:
        cp.wait_recv()

    def quad(xx):
        return pt.at[pl.ds(c * 16 + 4 * xx, 4)]

    cps = [push(quad(x), quad(x), gx_ss.at[k - 1], gx_rs.at[k - 1], x_peer(k)) for k in (1, 2, 3)]
    pcs = [push(quad(x), quad(x), gc_ss.at[0], gc_rs.at[0], partner)]
    for k in (1, 2, 3):
        cps[k - 1].wait_recv()
        src = quad(lax.rem(x + 4 - k, 4))
        pcs.append(push(src, src, gc_ss.at[k], gc_rs.at[k], partner))
    for cp in pcs:
        cp.wait_recv()

    acc = jnp.zeros((R, BLK), F32)
    for b in range(16):
        acc = acc + dot(jnp.concatenate([pt[2 * b], pt[2 * b + 1]], axis=1), xt[m, 256 * b : 256 * (b + 1), :])
    xpb[m] = acc.astype(BF)
    xp_cps = [push(xpb.at[m], xpb.at[m], xp_ss.at[k - 1], xp_rs.at[k - 1], mp_peer(k)) for k in range(1, 8)]

    below, above, across = lax.rem(z + 3, 4), lax.rem(z + 1, 4), lax.rem(z + 2, 4)
    pfs = []

    def hand_over(owner, j, idx):
        at_ = xt.at[2 * owner + c, rows(j)]
        pfs.append(push(at_, at_, pf_s.at[idx], pf_r.at[idx], partner))

    fwd = []
    for i in range(2):
        ring[("u", i)].wait_recv()
        s = xt.at[2 * below + c, rows(i)]
        fwd.append(push(s, s, fw_s.at[i], fw_r.at[i], z_peer(1)))
        ring[("d", 2 + i)].wait_recv()
        s = xt.at[2 * above + c, rows(2 + i)]
        fwd.append(push(s, s, fw_s.at[2 + i], fw_r.at[2 + i], z_peer(3)))
        hand_over(below, i, i)
        hand_over(above, 2 + i, 4 + 2 + i)

    gram = jnp.zeros((R, R), F32)
    for b in range(16):
        pp = jnp.concatenate([pt[2 * b], pt[2 * b + 1]], axis=1)
        gram = gram + dot(pp, pp, NT)

    for cp in xp_cps:
        cp.wait_recv()

    xpt = jnp.concatenate([xpb[i] for i in range(8)], axis=1)
    for n in range(7):
        part = dot(xpt, y_v[:, 256 * n : 256 * (n + 1)]) * (1.0 / 16.0)
        for h in range(2):
            for i in range(4):
                v = part[16 * i : 16 * (i + 1), BLK * h : BLK * (h + 1)]
                qf[i, 2 * n + h] = v
                qs[i, 2 * n + h] = v.astype(BF)
    cps = []
    for k in (1, 2, 3):
        to = lax.rem(x + k, 4)
        cps.append(push(qs.at[to], qx_r.at[k - 1], qx_ss.at[k - 1], qx_rs.at[k - 1], x_peer(k)))

    lane = lax.broadcasted_iota(jnp.int32, (R, 2 * R), 1)
    row = lax.broadcasted_iota(jnp.int32, (R, 2 * R), 0)
    eye = jnp.where(lane == row + R, 1.0, 0.0)
    work = jnp.concatenate([gram, jnp.zeros((R, R), F32)], axis=1) + eye

    def eliminate(j, w):
        rj = jnp.sum(jnp.where(row == j, w, 0.0), axis=0, keepdims=True)
        cj = jnp.sum(jnp.where(lane == j, w, 0.0), axis=1, keepdims=True)
        dj = jnp.sum(jnp.where(lane[:1] == j, rj, 0.0), axis=1, keepdims=True)
        f = jnp.where(row[:, :1] > j, cj / dj, 0.0)
        return w - f * rj

    work = lax.fori_loop(0, R, eliminate, work)
    diag = jnp.sum(jnp.where(lane == row, work, 0.0), axis=1, keepdims=True)
    linv[...] = work[:, R:] / jnp.sqrt(diag)

    tot = qf[x]
    for k in (1, 2, 3):
        cps[k - 1].wait_recv()
        tot = tot + qx_r[k - 1].astype(F32)
    qy_f[0:CB] = tot
    qy_f[CB:16] = jnp.zeros((2, 16, BLK), F32)
    qy_s[0:CB] = tot.astype(BF)
    qy_s[CB:16] = jnp.zeros((2, 16, BLK), BF)
    cps = []
    for k in (1, 2, 3):
        to = lax.rem(y + k, 4)
        cps.append(push(qy_s.at[pl.ds(4 * to, 4)], qy_r.at[k - 1], qy_ss.at[k - 1], qy_rs.at[k - 1], y_peer(k)))

    for i in range(2):
        ring[("u", 2 + i)].wait_recv()
        ring[("d", i)].wait_recv()
        hand_over(below, 2 + i, 2 + i)
        hand_over(above, i, 4 + i)

    tot = qy_f[pl.ds(4 * y, 4)]
    for k in (1, 2, 3):
        cps[k - 1].wait_recv()
        tot = tot + qy_r[k - 1].astype(F32)

    def mine(yy):
        return qa.at[x, pl.ds(4 * yy, 4)]

    qa[x, pl.ds(4 * y, 4)] = tot
    cps = [push(mine(y), mine(y), hy_ss.at[k - 1], hy_rs.at[k - 1], y_peer(k)) for k in (1, 2, 3)]

    for cp in pfs[:]:
        cp.wait_recv()
    for j in range(4):
        g_tile(below, j, False)

    for cp in cps:
        cp.wait_recv()
    cps = [push(qa.at[x], qa.at[x], hx_ss.at[k - 1], hx_rs.at[k - 1], x_peer(k)) for k in (1, 2, 3)]
    for j in range(4):
        g_tile(above, j, False)
    last = []
    for i in range(2):
        fwd[2 * i].wait_recv()
        fwd[2 * i + 1].wait_recv()
        hand_over(across, i, 8 + i)
        hand_over(across, 2 + i, 8 + 2 + i)
    for cp in cps:
        cp.wait_recv()

    li = linv[...]
    for b in range(7):
        raw = jnp.concatenate(
            [jnp.concatenate([qa[i, 2 * b + h] for i in range(4)], axis=0) for h in range(2)], axis=1
        )
        qt = dot3(li, raw)
        q_out[:, 256 * b : 256 * (b + 1)] = qt
        c_out[:, 256 * b : 256 * (b + 1)] = dot3(li, qt, TN).astype(BF)
    for b in range(NB):
        p_out[BLK * b : BLK * (b + 1), :] = pt[b].T

    for cp in pfs[8:]:
        cp.wait_recv()
    for j in range(4):
        g_tile(across, j, False)
    for cp in sent:
        cp.wait_send()


def finish_kernel(g0, g1, g2, g3, p_ref, q_ref, c_ref, e_ref, q_out):
    i = pl.program_id(0)
    q_out[...] = q_ref[...]
    at_row = pl.multiple_of(lax.rem(i, 2) * 512, 512)
    for s, g in enumerate((g0, g1, g2, g3)):

        @pl.when(i // 2 == s)
        def _(g=g):
            p = p_ref[pl.ds(pl.multiple_of(i * 512, 512), 512), :]
            for n in range(7):
                cols = slice(256 * n, 256 * (n + 1))
                e_ref[:, cols] = (g[pl.ds(at_row, 512), cols] - dot(p, c_ref[:, cols])).astype(BF)


def per_device(activations, output_grads, q_start):
    vm = pl.BlockSpec(memory_space=pltpu.VMEM)
    dma = pltpu.SemaphoreType.DMA
    outs = pl.pallas_call(
        factor_kernel,
        out_shape=[jax.ShapeDtypeStruct((ROWS, FFL), F32)] * 4
        + [
            jax.ShapeDtypeStruct((D, R), BF),
            jax.ShapeDtypeStruct((R, FFL), F32),
            jax.ShapeDtypeStruct((R, FFL), BF),
        ],
        in_specs=[pl.BlockSpec(memory_space=pl.ANY)] * 3,
        out_specs=[vm] * 7,
        scratch_shapes=[
            pltpu.VMEM((128, D), BF),
            pltpu.VMEM((TOK, FFL), BF),
            pltpu.VMEM((R, FFL), F32),
            pltpu.VMEM((8, D, 128), BF),
            pltpu.VMEM((8, R, BLK), F32),
            pltpu.VMEM((8, R, BLK), BF),
            pltpu.VMEM((7, R, BLK), BF),
            pltpu.VMEM((16, R, BLK), F32),
            pltpu.VMEM((16, R, BLK), BF),
            pltpu.VMEM((16, R, BLK), BF),
            pltpu.VMEM((16, R, BLK), BF),
            pltpu.VMEM((3, 4, R, BLK), BF),
            pltpu.VMEM((4, R, BLK), F32),
            pltpu.VMEM((4, R, BLK), BF),
            pltpu.VMEM((3, R, BLK), BF),
            pltpu.VMEM((4, R, BLK), F32),
            pltpu.VMEM((NB, R, BLK), BF),
            pltpu.VMEM((8, R, BLK), BF),
            pltpu.VMEM((4, CB, 16, BLK), F32),
            pltpu.VMEM((4, CB, 16, BLK), BF),
            pltpu.VMEM((3, CB, 16, BLK), BF),
            pltpu.VMEM((16, 16, BLK), F32),
            pltpu.VMEM((16, 16, BLK), BF),
            pltpu.VMEM((3, 4, 16, BLK), BF),
            pltpu.VMEM((4, 16, 16, BLK), F32),
            pltpu.VMEM((R, R), F32),
            dma((6,)),
            dma((7,)), dma((7,)),
            dma((1,)), dma((1,)),
            dma((3,)), dma((3,)),
            dma((3,)), dma((3,)),
            dma((3,)), dma((3,)),
            dma((3,)), dma((3,)),
            dma((3,)), dma((3,)),
            dma((4,)), dma((4,)),
            dma((7,)), dma((7,)),
            dma((3,)), dma((3,)),
            dma((3,)), dma((3,)),
            dma((3,)), dma((3,)),
            dma((3,)), dma((3,)),
            dma((1,)), dma((1,)),
            dma((4,)), dma((4,)),
            dma((4,)), dma((4,)),
            dma((4,)), dma((4,)),
            dma((12,)), dma((12,)),
        ],
        compiler_params=pltpu.CompilerParams(collective_id=0, has_side_effects=True, vmem_limit_bytes=20 * 2**20),
        name="factors",
    )(
        pltpu.with_memory_space_constraint(activations, pltpu.HBM),
        pltpu.with_memory_space_constraint(output_grads, pltpu.HBM),
        pltpu.with_memory_space_constraint(q_start.T, pltpu.HBM),
    )
    new_error, q_factor = pl.pallas_call(
        finish_kernel,
        grid=(8,),
        out_shape=(jax.ShapeDtypeStruct((D, FFL), BF), jax.ShapeDtypeStruct((R, FFL), F32)),
        in_specs=[vm] * 7,
        out_specs=(pl.BlockSpec((512, FFL), lambda i: (i, 0)), pl.BlockSpec((R, FFL), lambda i: (0, 0))),
        compiler_params=pltpu.CompilerParams(vmem_limit_bytes=12 * 2**20),
        name="finish",
    )(*outs)
    return new_error, q_factor.T


def solution(mesh):
    in_specs = (P(("dp", "mp"), None), P("dp", "mp"), P("mp", None))
    out_specs = (P("dp", "mp"), P("mp", None))
    return jax.shard_map(per_device, mesh=mesh, in_specs=in_specs, out_specs=out_specs, check_vma=False)
```

time: 295 us -> 84.9 us (0.29)
  waiting for transfers between devices: 130 us -> 0 us
  Pallas kernels: 0 us -> 84.1 us
  matrix products: 67 us -> 0 us
  blocking collectives: 61.4 us -> 0 us
  other arithmetic: 14.3 us -> 0 us
  between operations: 14.2 us -> 0.64 us
  starting transfers between devices: 4.3 us -> 0 us
    pallas_call x0 -> x2, Pallas kernels: none -> 84.1 us  [the longest x1 75.8 us: per_device(): pl.pallas_call(factor_kernel, out_shape=[jax.ShapeDtypeStruct((ROWS, FFL)...]
    psum x1 -> x0, waiting for transfers between devices: 80.5 us -> none  [per_device(): q_factor = lax.psum(local_factor, 'dp') / replicas]
    dot_general x8 -> x0, matrix products: 66.7 us -> none  [the longest x1 22.9 us: per_device(): lax.dot_general(gathered, output_grads, contract_rows, preferred_element_...]
    all_to_all x3 -> x0, blocking collectives: 61.4 us -> none  [the longest x2 43.2 us: copy_for_each(): lax.all_to_all(jnp.broadcast_to(value[None], (count, *value.shape)), axis...]
    all_gather x1 -> x0, waiting for transfers between devices: 48.4 us -> none  [per_device(): gathered = lax.all_gather(activations, 'mp', axis=0, tiled=True)]
    another operation x5 -> x0, other arithmetic: 12.1 us -> none  [the longest x3 6.52 us: orthonormal(): lower_tri = jnp.linalg.cholesky(gram_matrix)]
    all_to_all x1 -> x0, starting transfers between devices: 4.26 us -> none  [copy_for_each(): lax.all_to_all(jnp.broadcast_to(value[None], (count, *value.shape)), axis...]
  transfers between devices with their start and end apart: 3 -> 0, of which waited for: 2 -> 0; matrix products, arithmetic and copies ran while one was open for 10% -> 0% of each run, Pallas kernels for 0% -> 0%
where the time goes in v1:
time: 84.9 us; the launch traced here: 84.8 us
  Pallas kernels  84.1 us (99%)
    pallas_call x1, Pallas kernels, per_device(): pl.pallas_call(factor_kernel, out_shape=[jax.ShapeDtypeStruct((ROWS, FFL)...  75.8 us
    pallas_call x1, Pallas kernels, per_device(): pl.pallas_call(finish_kernel, grid=(8,), out_shape=(jax.ShapeDtypeStruct(...  8.3 us

profile of v1, /device:TPU:1, one launch (start us, length us, event | category | flops | bytes accessed | tf_op | source)
XLA Modules:
  0.0 84.8 jit_solution(7888033922750678244)
XLA Ops:
  0.6 75.8 %factors.1 = (f32[1024,1792]{1,0:T(8,128)S(1)}, f32[1024,1792]{1,0:T(8,128)S(1)}, f32[1024,1792]{1,0:T(8,128)S(1)}, f32[1024,1792]{1,0:T(8,128)S(1)}, bf16[4096,...) custom-call(bf16[128,4096]{1,0:T(8,128)(2,1)} %x_hbm.1, bf16[1024,1792]{1,0:T(8,128)(2,1)} %y_hbm.1, ...), custom_call_target="tpu_custom_call" | custom-call | tf_op jit(solution)/shard_map/factors/pallas_call | solution.py:360
  76.5 8.3 %finish.1 = (bf16[4096,1792]{1,0:T(8,128)(2,1)}, f32[64,1792]{1,0:T(8,128)}) custom-call(f32[1024,1792]{1,0:T(8,128)S(1)} %get-tuple-element.11.g0, f32[1024,1792]{1,0:T(8,128)S(1)} %get-tuple-element.12.g1, f32[1024,1792]{1,0:T(8,128)S(1)} %get-tuple-element.13.g2, f32[1024,1792]{1,0:T(8,128)S(1)} %get-tuple-element.14.g3, ...), custom_call_target="tpu_custom_call" | custom-call | tf_op jit(solution)/shard_map/finish/pallas_call | solution.py:424

commit v2 on v1

v2 whole, which is shorter than its diff:
```python
import jax
import jax.numpy as jnp
from jax import lax
from jax.experimental import pallas as pl
from jax.experimental.pallas import tpu as pltpu
from jax.sharding import PartitionSpec as P

MESH = pl.DeviceIdType.MESH
BF, F32 = jnp.bfloat16, jnp.float32
D, FFL, R, TOK = 4096, 1792, 64, 1024
BLK, NB = 128, 32
ROWS = 1024
FAR_FIRST = sorted(range(1, 16), key=lambda o: -(min(o // 4, 4 - o // 4) + min(o % 4, 4 - o % 4)))
NN = (((1,), (0,)), ((), ()))
NT = (((1,), (1,)), ((), ()))
TN = (((0,), (0,)), ((), ()))


def dot(a, b, dims=NN):
    return lax.dot_general(a, b, dims, preferred_element_type=F32)


def halves(v):
    upper = v.astype(BF)
    return upper, (v - upper.astype(F32)).astype(BF)


def dot3(a, b, dims=NN):
    (ah, al), (bh, bl) = halves(a), halves(b)
    return dot(ah, bh, dims) + (dot(ah, bl, dims) + dot(al, bh, dims))


def factor_kernel(
    x_hbm, y_hbm, q_hbm, g0, g1, g2, g3, p_out, q_out, c_out,
    x_v, y_v, q_v, xt, af, a_s, a_r, pown, pc_s, pc_r, px_s, px_r, pz, pt, xpb, qf, qs, q_r, qa, linv,
    ld_sem, a_ss, a_rs, c_ss, c_rs, p_ss, p_rs, z_ss, z_rs, gp_ss, gp_rs, gc_ss, gc_rs, xp_ss, xp_rs,
    q_ss, q_rs, gq_ss, gq_rs, own_s, own_r, up_s, up_r, dn_s, dn_r, fw_s, fw_r, pf_s, pf_r,
):
    g_refs = (g0, g1, g2, g3)
    r, m = lax.axis_index("dp"), lax.axis_index("mp")
    z, c = m // 2, lax.rem(m, 2)
    partner = {"dp": r, "mp": z * 2 + (1 - c)}

    def mp_peer(k):
        return {"dp": r, "mp": lax.rem(m + k, 8)}

    def dp_peer(k):
        return {"dp": lax.rem(r + k, 16), "mp": m}

    def z_peer(k):
        return {"dp": r, "mp": lax.rem(z + k, 4) * 2 + c}

    sent = []

    def push(src, dst, ssem, rsem, dev):
        cp = pltpu.make_async_remote_copy(
            src_ref=src, dst_ref=dst, send_sem=ssem, recv_sem=rsem, device_id=dev, device_id_type=MESH
        )
        cp.start()
        sent.append(cp)
        return cp

    q_cp = pltpu.make_async_copy(q_hbm, q_v, ld_sem.at[1])
    x_cp = pltpu.make_async_copy(x_hbm, x_v, ld_sem.at[0])
    y_cps = [
        pltpu.make_async_copy(y_hbm.at[pl.ds(256 * i, 256)], y_v.at[pl.ds(256 * i, 256)], ld_sem.at[2 + i])
        for i in range(4)
    ]
    q_cp.start()
    for cp in y_cps:
        cp.start()
    x_cp.start()

    bar = pltpu.get_barrier_semaphore()
    for dev in [mp_peer(k) for k in range(1, 8)] + [dp_peer(k) for k in range(1, 16)]:
        pl.semaphore_signal(bar, inc=1, device_id=dev, device_id_type=MESH)

    q_cp.wait()
    qh, ql = halves(q_v[...])
    qq = jnp.concatenate([qh, ql], axis=0)
    for i in range(4):
        y_cps[i].wait()
        both = dot(qq, y_v[256 * i : 256 * (i + 1), :], NT)
        at = both[:R] + both[R:]
        for h in range(2):
            blk = at[:, BLK * h : BLK * (h + 1)]
            af[2 * i + h] = blk
            a_s[2 * i + h] = blk.astype(BF)
    pl.semaphore_wait(bar, 22)
    a_cps = []
    for k in (4, 3, 5, 2, 6, 1, 7):
        to = lax.rem(m + k, 8)
        a_cps.append(push(a_s.at[to], a_r.at[k - 1], a_ss.at[k - 1], a_rs.at[k - 1], mp_peer(k)))

    x_cp.wait()
    for i in range(4):
        xt[m, 1024 * i : 1024 * (i + 1), :] = x_v[:, 1024 * i : 1024 * (i + 1)].T
    own = push(xt.at[m], xt.at[m], own_s.at[0], own_r.at[0], partner)

    def rows(j):
        return pl.ds(ROWS * j, ROWS)

    ring = {}

    def ring_own(i):
        for key, j, ss, rs, k in (("u", i, up_s, up_r, 1), ("d", (i + 2) % 4, dn_s, dn_r, 3)):
            here = xt.at[m, rows(j)]
            ring[key, j] = push(here, here, ss.at[j], rs.at[j], z_peer(k))

    below, above, across = lax.rem(z + 3, 4), lax.rem(z + 1, 4), lax.rem(z + 2, 4)
    pfs = {}

    def hand_over(name, owner, j, idx):
        here = xt.at[2 * owner + c, rows(j)]
        pfs[name, j] = push(here, here, pf_s.at[idx], pf_r.at[idx], partner)

    def arrived(i):
        j = (i + 2) % 4
        ring["u", i].wait_recv()
        hand_over("below", below, i, i)
        ring["d", j].wait_recv()
        hand_over("above", above, j, 4 + j)

    fwd = {}

    def forward(i):
        j = i + 2
        here = xt.at[2 * below + c, rows(i)]
        fwd[i] = push(here, here, fw_s.at[i], fw_r.at[i], z_peer(1))
        here = xt.at[2 * above + c, rows(j)]
        fwd[j] = push(here, here, fw_s.at[j], fw_r.at[j], z_peer(3))

    def arrived_far(i):
        for j in (i, i + 2):
            fwd[j].wait_recv()
            hand_over("across", across, j, 8 + j)

    ring_own(0)
    ring_own(1)

    def g_tile(zz, j, first=False):
        def body(h, carry):
            at_row = pl.multiple_of(512 * h, 512)
            src = pl.multiple_of(ROWS * j + 512 * h, 512)
            lhs = jnp.concatenate([xt[2 * zz, pl.ds(src, 512), :], xt[2 * zz + 1, pl.ds(src, 512), :]], axis=1)
            for n in range(7):
                w = y_v[pl.ds(pl.multiple_of(256 * zz, 256), 256), 256 * n : 256 * (n + 1)]
                prod = dot(lhs, w)
                spot = (pl.ds(at_row, 512), slice(256 * n, 256 * (n + 1)))
                if first:
                    g_refs[j][spot] = prod
                else:
                    g_refs[j][spot] = g_refs[j][spot] + prod
            return carry

        lax.fori_loop(0, 2, body, 0)

    def g_far(name, zz, j):
        pfs[name, j].wait_recv()
        g_tile(zz, j)

    at = af[m]
    for cp in a_cps:
        cp.wait_recv()
    for k in range(1, 8):
        at = at + a_r[k - 1].astype(F32)

    ath, atl = halves(at)
    aa = jnp.concatenate([ath, atl], axis=0)

    def p_part(half, write):
        for b in range(8):
            col = pl.multiple_of(half * 2048 + 256 * b, 256)
            both = dot(aa, x_v[:, pl.ds(col, 256)])
            s = both[:R] + both[R:]
            write(2 * b, s[:, :BLK])
            write(2 * b + 1, s[:, BLK:])

    def put_send(b, v):
        pc_s[b] = v.astype(BF)

    def put_own(b, v):
        pown[b] = v

    p_part(1 - c, put_send)
    pc = push(pc_s, pc_r, c_ss.at[0], c_rs.at[0], partner)
    p_part(c, put_own)
    own.wait_recv()
    g_tile(z, 0, True)
    pc.wait_recv()
    tot = pown[...] + pc_r[...].astype(F32)
    pown[...] = tot
    px_s[...] = tot.astype(BF)
    cps = []
    for k in FAR_FIRST:
        to = lax.rem(r + k, 16)
        cps.append(push(px_s.at[to], px_r.at[k - 1], p_ss.at[k - 1], p_rs.at[k - 1], dp_peer(k)))
    for j in range(1, 4):
        g_tile(z, j, True)
    arrived(0)
    for cp in cps:
        cp.wait_recv()
    tot = pown[r]
    for k in range(1, 16):
        tot = tot + px_r[k - 1].astype(F32)
    pz[z] = tot * (1.0 / 16.0)
    cps = [push(pz.at[z], pz.at[z], z_ss.at[k - 1], z_rs.at[k - 1], z_peer(k)) for k in (2, 1, 3)]
    ring_own(2)
    g_far("below", below, 0)
    g_far("above", above, 2)
    for cp in cps:
        cp.wait_recv()
    blk = c * 16 + r
    pt[blk] = ((pz[0] + pz[1]) + (pz[2] + pz[3])).astype(BF)

    cps = [(k, push(pt.at[blk], pt.at[blk], gp_ss.at[k - 1], gp_rs.at[k - 1], dp_peer(k))) for k in FAR_FIRST]
    pcs = [push(pt.at[blk], pt.at[blk], gc_ss.at[0], gc_rs.at[0], partner)]
    ring_own(3)
    arrived(1)
    g_far("below", below, 1)
    g_far("above", above, 3)
    for k, cp in reversed(cps):
        cp.wait_recv()
        here = pt.at[c * 16 + lax.rem(r + 16 - k, 16)]
        pcs.append(push(here, here, gc_ss.at[k], gc_rs.at[k], partner))
    for cp in pcs:
        cp.wait_recv()

    acc = jnp.zeros((R, BLK), F32)
    for b in range(16):
        acc = acc + dot(jnp.concatenate([pt[2 * b], pt[2 * b + 1]], axis=1), xt[m, 256 * b : 256 * (b + 1), :])
    xpb[m] = acc.astype(BF)
    xp_cps = [push(xpb.at[m], xpb.at[m], xp_ss.at[k - 1], xp_rs.at[k - 1], mp_peer(k)) for k in (4, 3, 5, 2, 6, 1, 7)]
    forward(0)
    forward(1)
    arrived(2)

    gram = jnp.zeros((R, R), F32)
    for b in range(16):
        pp = jnp.concatenate([pt[2 * b], pt[2 * b + 1]], axis=1)
        gram = gram + dot(pp, pp, NT)
    g_far("below", below, 2)
    g_far("above", above, 0)

    for cp in xp_cps:
        cp.wait_recv()

    xpt = jnp.concatenate([xpb[i] for i in range(8)], axis=1)
    for i in range(4):
        qs[4 * i + 3, 2:4] = jnp.zeros((2, 16, BLK), BF)
        qf[4 * i + 3, 2:4] = jnp.zeros((2, 16, BLK), F32)
    for n in range(7):
        part = dot(xpt, y_v[:, 256 * n : 256 * (n + 1)]) * (1.0 / 16.0)
        for h in range(2):
            cb = 2 * n + h
            for i in range(4):
                v = part[16 * i : 16 * (i + 1), BLK * h : BLK * (h + 1)]
                qf[4 * i + cb // 4, cb % 4] = v
                qs[4 * i + cb // 4, cb % 4] = v.astype(BF)
    cps = []
    for k in FAR_FIRST:
        to = lax.rem(r + k, 16)
        cps.append(push(qs.at[to], q_r.at[k - 1], q_ss.at[k - 1], q_rs.at[k - 1], dp_peer(k)))
    arrived(3)

    lane = lax.broadcasted_iota(jnp.int32, (R, 2 * R), 1)
    row = lax.broadcasted_iota(jnp.int32, (R, 2 * R), 0)
    eye = jnp.where(lane == row + R, 1.0, 0.0)
    work = jnp.concatenate([gram, jnp.zeros((R, R), F32)], axis=1) + eye

    def eliminate(j, w):
        rj = jnp.sum(jnp.where(row == j, w, 0.0), axis=0, keepdims=True)
        cj = jnp.sum(jnp.where(lane == j, w, 0.0), axis=1, keepdims=True)
        dj = jnp.sum(jnp.where(lane[:1] == j, rj, 0.0), axis=1, keepdims=True)
        f = jnp.where(row[:, :1] > j, cj / dj, 0.0)
        return w - f * rj

    work = lax.fori_loop(0, R, eliminate, work)
    diag = jnp.sum(jnp.where(lane == row, work, 0.0), axis=1, keepdims=True)
    linv[...] = work[:, R:] / jnp.sqrt(diag)

    for cp in cps:
        cp.wait_recv()
    tot = qf[r]
    for k in range(1, 16):
        tot = tot + q_r[k - 1].astype(F32)
    qa[r] = tot.astype(BF)
    cps = [push(qa.at[r], qa.at[r], gq_ss.at[k - 1], gq_rs.at[k - 1], dp_peer(k)) for k in FAR_FIRST]

    g_far("below", below, 3)
    g_far("above", above, 1)
    arrived_far(0)
    for b in range(NB):
        p_out[BLK * b : BLK * (b + 1), :] = pt[b].T
    g_far("across", across, 0)
    g_far("across", across, 2)
    arrived_far(1)
    for cp in cps:
        cp.wait_recv()

    lh, ll = halves(linv[...])
    for b in range(7):
        raw = jnp.concatenate(
            [
                jnp.concatenate([qa[4 * i + cb // 4, cb % 4] for i in range(4)], axis=0)
                for cb in (2 * b, 2 * b + 1)
            ],
            axis=1,
        )
        qt = dot(lh, raw) + dot(ll, raw)
        q_out[:, 256 * b : 256 * (b + 1)] = qt
        c_out[:, 256 * b : 256 * (b + 1)] = dot3(linv[...], qt, TN).astype(BF)

    g_far("across", across, 1)
    g_far("across", across, 3)
    for cp in sent:
        cp.wait_send()


def finish_kernel(g0, g1, g2, g3, p_ref, q_ref, c_ref, e_ref, q_out):
    i = pl.program_id(0)
    q_out[...] = q_ref[...]
    at_row = pl.multiple_of(lax.rem(i, 2) * 512, 512)
    for s, g in enumerate((g0, g1, g2, g3)):

        @pl.when(i // 2 == s)
        def _(g=g):
            p = p_ref[pl.ds(pl.multiple_of(i * 512, 512), 512), :]
            for n in range(7):
                cols = slice(256 * n, 256 * (n + 1))
                e_ref[:, cols] = (g[pl.ds(at_row, 512), cols] - dot(p, c_ref[:, cols])).astype(BF)


def per_device(activations, output_grads, q_start):
    vm = pl.BlockSpec(memory_space=pltpu.VMEM)
    dma = pltpu.SemaphoreType.DMA
    outs = pl.pallas_call(
        factor_kernel,
        out_shape=[jax.ShapeDtypeStruct((ROWS, FFL), F32)] * 4
        + [
            jax.ShapeDtypeStruct((D, R), BF),
            jax.ShapeDtypeStruct((R, FFL), F32),
            jax.ShapeDtypeStruct((R, FFL), BF),
        ],
        in_specs=[pl.BlockSpec(memory_space=pl.ANY)] * 3,
        out_specs=[vm] * 7,
        scratch_shapes=[
            pltpu.VMEM((128, D), BF),
            pltpu.VMEM((TOK, FFL), BF),
            pltpu.VMEM((R, FFL), F32),
            pltpu.VMEM((8, D, 128), BF),
            pltpu.VMEM((8, R, BLK), F32),
            pltpu.VMEM((8, R, BLK), BF),
            pltpu.VMEM((7, R, BLK), BF),
            pltpu.VMEM((16, R, BLK), F32),
            pltpu.VMEM((16, R, BLK), BF),
            pltpu.VMEM((16, R, BLK), BF),
            pltpu.VMEM((16, R, BLK), BF),
            pltpu.VMEM((15, R, BLK), BF),
            pltpu.VMEM((4, R, BLK), F32),
            pltpu.VMEM((NB, R, BLK), BF),
            pltpu.VMEM((8, R, BLK), BF),
            pltpu.VMEM((16, 4, 16, BLK), F32),
            pltpu.VMEM((16, 4, 16, BLK), BF),
            pltpu.VMEM((15, 4, 16, BLK), BF),
            pltpu.VMEM((16, 4, 16, BLK), BF),
            pltpu.VMEM((R, R), F32),
            dma((6,)),
            dma((7,)), dma((7,)),
            dma((1,)), dma((1,)),
            dma((15,)), dma((15,)),
            dma((3,)), dma((3,)),
            dma((15,)), dma((15,)),
            dma((16,)), dma((16,)),
            dma((7,)), dma((7,)),
            dma((15,)), dma((15,)),
            dma((15,)), dma((15,)),
            dma((1,)), dma((1,)),
            dma((4,)), dma((4,)),
            dma((4,)), dma((4,)),
            dma((4,)), dma((4,)),
            dma((12,)), dma((12,)),
        ],
        compiler_params=pltpu.CompilerParams(collective_id=0, has_side_effects=True, vmem_limit_bytes=20 * 2**20),
        name="factors",
    )(
        pltpu.with_memory_space_constraint(activations, pltpu.HBM),
        pltpu.with_memory_space_constraint(output_grads, pltpu.HBM),
        pltpu.with_memory_space_constraint(q_start.T, pltpu.HBM),
    )
    new_error, q_factor = pl.pallas_call(
        finish_kernel,
        grid=(8,),
        out_shape=(jax.ShapeDtypeStruct((D, FFL), BF), jax.ShapeDtypeStruct((R, FFL), F32)),
        in_specs=[vm] * 7,
        out_specs=(pl.BlockSpec((512, FFL), lambda i: (i, 0)), pl.BlockSpec((R, FFL), lambda i: (0, 0))),
        compiler_params=pltpu.CompilerParams(vmem_limit_bytes=12 * 2**20),
        name="finish",
    )(*outs)
    return new_error, q_factor.T


def solution(mesh):
    in_specs = (P(("dp", "mp"), None), P("dp", "mp"), P("mp", None))
    out_specs = (P("dp", "mp"), P("mp", None))
    return jax.shard_map(per_device, mesh=mesh, in_specs=in_specs, out_specs=out_specs, check_vma=False)
```

time: 84.9 us -> 68.2 us (0.80)
  Pallas kernels: 84.1 us -> 67.5 us
    pallas_call x1, Pallas kernels: 75.8 us -> 59.1 us  [per_device(): pl.pallas_call(factor_kernel, out_shape=[jax.ShapeDtypeStruct((ROWS, FFL)...]
where the time goes in v2:
time: 68.2 us; the launch traced here: 68.1 us
  Pallas kernels  67.5 us (99%)
    pallas_call x1, Pallas kernels, per_device(): pl.pallas_call(factor_kernel, out_shape=[jax.ShapeDtypeStruct((ROWS, FFL)...  59.1 us
    pallas_call x1, Pallas kernels, per_device(): pl.pallas_call(finish_kernel, grid=(8,), out_shape=(jax.ShapeDtypeStruct(...  8.31 us

profile of v2, /device:TPU:1, one launch (start us, length us, event | category | flops | bytes accessed | tf_op | source)
XLA Modules:
  0.0 68.1 jit_solution(16136981127698679835)
XLA Ops:
  0.6 59.1 %factors.1 = (f32[1024,1792]{1,0:T(8,128)S(1)}, f32[1024,1792]{1,0:T(8,128)S(1)}, f32[1024,1792]{1,0:T(8,128)S(1)}, f32[1024,1792]{1,0:T(8,128)S(1)}, bf16[4096,...) custom-call(bf16[128,4096]{1,0:T(8,128)(2,1)} %x_hbm.1, bf16[1024,1792]{1,0:T(8,128)(2,1)} %y_hbm.1, ...), custom_call_target="tpu_custom_call" | custom-call | tf_op jit(solution)/shard_map/factors/pallas_call | solution.py:337
  59.8 8.3 %finish.1 = (bf16[4096,1792]{1,0:T(8,128)(2,1)}, f32[64,1792]{1,0:T(8,128)}) custom-call(f32[1024,1792]{1,0:T(8,128)S(1)} %get-tuple-element.11.g0, f32[1024,1792]{1,0:T(8,128)S(1)} %get-tuple-element.12.g1, f32[1024,1792]{1,0:T(8,128)S(1)} %get-tuple-element.13.g2, f32[1024,1792]{1,0:T(8,128)S(1)} %get-tuple-element.14.g3, ...), custom_call_target="tpu_custom_call" | custom-call | tf_op jit(solution)/shard_map/finish/pallas_call | solution.py:391

commit v3 on v2

--- a/solution.py
+++ b/solution.py
@@ -10,6 +10,7 @@
 D, FFL, R, TOK = 4096, 1792, 64, 1024
 BLK, NB = 128, 32
 ROWS = 1024
+PIECES = 8
 FAR_FIRST = sorted(range(1, 16), key=lambda o: -(min(o // 4, 4 - o // 4) + min(o % 4, 4 - o % 4)))
 NN = (((1,), (0,)), ((), ()))
 NT = (((1,), (1,)), ((), ()))
@@ -66,36 +67,18 @@
         pltpu.make_async_copy(y_hbm.at[pl.ds(256 * i, 256)], y_v.at[pl.ds(256 * i, 256)], ld_sem.at[2 + i])
         for i in range(4)
     ]
+    x_cp.start()
     q_cp.start()
     for cp in y_cps:
         cp.start()
-    x_cp.start()
 
     bar = pltpu.get_barrier_semaphore()
     for dev in [mp_peer(k) for k in range(1, 8)] + [dp_peer(k) for k in range(1, 16)]:
         pl.semaphore_signal(bar, inc=1, device_id=dev, device_id_type=MESH)
 
-    q_cp.wait()
-    qh, ql = halves(q_v[...])
-    qq = jnp.concatenate([qh, ql], axis=0)
-    for i in range(4):
-        y_cps[i].wait()
-        both = dot(qq, y_v[256 * i : 256 * (i + 1), :], NT)
-        at = both[:R] + both[R:]
-        for h in range(2):
-            blk = at[:, BLK * h : BLK * (h + 1)]
-            af[2 * i + h] = blk
-            a_s[2 * i + h] = blk.astype(BF)
-    pl.semaphore_wait(bar, 22)
-    a_cps = []
-    for k in (4, 3, 5, 2, 6, 1, 7):
-        to = lax.rem(m + k, 8)
-        a_cps.append(push(a_s.at[to], a_r.at[k - 1], a_ss.at[k - 1], a_rs.at[k - 1], mp_peer(k)))
-
     x_cp.wait()
     for i in range(4):
         xt[m, 1024 * i : 1024 * (i + 1), :] = x_v[:, 1024 * i : 1024 * (i + 1)].T
-    own = push(xt.at[m], xt.at[m], own_s.at[0], own_r.at[0], partner)
 
     def rows(j):
         return pl.ds(ROWS * j, ROWS)
@@ -117,8 +100,8 @@
     def arrived(i):
         j = (i + 2) % 4
         ring["u", i].wait_recv()
+        ring["d", j].wait_recv()
         hand_over("below", below, i, i)
-        ring["d", j].wait_recv()
         hand_over("above", above, j, 4 + j)
 
     fwd = {}
@@ -135,22 +118,45 @@
             fwd[j].wait_recv()
             hand_over("across", across, j, 8 + j)
 
+    q_cp.wait()
+    qh, ql = halves(q_v[...])
+    qq = jnp.concatenate([qh, ql], axis=0)
+    for first, count in ((0, 2), (2, 6)):
+        for cp in y_cps[first // 2 : (first + count) // 2]:
+            cp.wait()
+        both = dot(qq, y_v[BLK * first : BLK * (first + count), :], NT)
+        at = both[:R] + both[R:]
+        for h in range(count):
+            blk = at[:, BLK * h : BLK * (h + 1)]
+            af[first + h] = blk
+            a_s[first + h] = blk.astype(BF)
+    pl.semaphore_wait(bar, 22)
+    a_cps = []
+    for k in (4, 3, 5, 2, 6, 1, 7):
+        to = lax.rem(m + k, 8)
+        a_cps.append(push(a_s.at[to], a_r.at[k - 1], a_ss.at[k - 1], a_rs.at[k - 1], mp_peer(k)))
+
+    own = push(xt.at[m], xt.at[m], own_s.at[0], own_r.at[0], partner)
     ring_own(0)
     ring_own(1)
 
     def g_tile(zz, j, first=False):
+        w_rows = pl.ds(pl.multiple_of(256 * zz, 256), 256)
+
+        def part(here, there):
+            lhs = jnp.concatenate([xt[2 * zz, here, :], xt[2 * zz + 1, here, :]], axis=1)
+            for n in range(7):
+                cols = slice(256 * n, 256 * (n + 1))
+                prod = dot(lhs, y_v[w_rows, cols])
+                g_refs[j][there, cols] = prod if first else g_refs[j][there, cols] + prod
+
+        if first:
+            part(rows(j), slice(None))
+            return
+
         def body(h, carry):
             at_row = pl.multiple_of(512 * h, 512)
-            src = pl.multiple_of(ROWS * j + 512 * h, 512)
-            lhs = jnp.concatenate([xt[2 * zz, pl.ds(src, 512), :], xt[2 * zz + 1, pl.ds(src, 512), :]], axis=1)
-            for n in range(7):
-                w = y_v[pl.ds(pl.multiple_of(256 * zz, 256), 256), 256 * n : 256 * (n + 1)]
-                prod = dot(lhs, w)
-                spot = (pl.ds(at_row, 512), slice(256 * n, 256 * (n + 1)))
-                if first:
-                    g_refs[j][spot] = prod
-                else:
-                    g_refs[j][spot] = g_refs[j][spot] + prod
+            part(pl.ds(pl.multiple_of(ROWS * j + at_row, 512), 512), pl.ds(at_row, 512))
             return carry
 
         lax.fori_loop(0, 2, body, 0)
@@ -208,6 +214,7 @@
     ring_own(2)
     g_far("below", below, 0)
     g_far("above", above, 2)
+    arrived(1)
     for cp in cps:
         cp.wait_recv()
     blk = c * 16 + r
@@ -216,7 +223,6 @@
     cps = [(k, push(pt.at[blk], pt.at[blk], gp_ss.at[k - 1], gp_rs.at[k - 1], dp_peer(k))) for k in FAR_FIRST]
     pcs = [push(pt.at[blk], pt.at[blk], gc_ss.at[0], gc_rs.at[0], partner)]
     ring_own(3)
-    arrived(1)
     g_far("below", below, 1)
     g_far("above", above, 3)
     for k, cp in reversed(cps):
@@ -233,15 +239,39 @@
     xp_cps = [push(xpb.at[m], xpb.at[m], xp_ss.at[k - 1], xp_rs.at[k - 1], mp_peer(k)) for k in (4, 3, 5, 2, 6, 1, 7)]
     forward(0)
     forward(1)
-    arrived(2)
 
     gram = jnp.zeros((R, R), F32)
     for b in range(16):
         pp = jnp.concatenate([pt[2 * b], pt[2 * b + 1]], axis=1)
         gram = gram + dot(pp, pp, NT)
-    g_far("below", below, 2)
-    g_far("above", above, 0)
-
+    arrived(2)
+    lane = lax.broadcasted_iota(jnp.int32, (R, 2 * R), 1)
+    row = lax.broadcasted_iota(jnp.int32, (R, 2 * R), 0)
+    eye = jnp.where(lane == row + R, 1.0, 0.0)
+    work = jnp.concatenate([gram, jnp.zeros((R, R), F32)], axis=1) + eye
+
+    def eliminate(i, w):
+        j = 2 * i
+        r1 = jnp.sum(jnp.where(row == j, w, 0.0), axis=0, keepdims=True)
+        r2 = jnp.sum(jnp.where(row == j + 1, w, 0.0), axis=0, keepdims=True)
+        c1 = jnp.sum(jnp.where(lane == j, w, 0.0), axis=1, keepdims=True)
+        c2 = jnp.sum(jnp.where(lane == j + 1, w, 0.0), axis=1, keepdims=True)
+        da = jnp.sum(jnp.where(lane[:1] == j, r1, 0.0), axis=1, keepdims=True)
+        db = jnp.sum(jnp.where(lane[:1] == j + 1, r1, 0.0), axis=1, keepdims=True)
+        dc = jnp.sum(jnp.where(lane[:1] == j + 1, r2, 0.0), axis=1, keepdims=True)
+        inv = 1.0 / da
+        ratio = db * inv
+        f2 = (c2 - ratio * c1) / (dc - ratio * db)
+        f1 = (c1 - db * f2) * inv
+        f1 = jnp.where(row[:, :1] > j + 1, f1, jnp.where(row[:, :1] == j + 1, ratio, 0.0))
+        f2 = jnp.where(row[:, :1] > j + 1, f2, 0.0)
+        return w - (f1 * r1 + f2 * r2)
+
+    work = lax.fori_loop(0, R // 2, eliminate, work)
+    diag = jnp.sum(jnp.where(lane == row, work, 0.0), axis=1, keepdims=True)
+    linv[...] = work[:, R:] / jnp.sqrt(diag)
+
+    arrived(3)
     for cp in xp_cps:
         cp.wait_recv()
 
@@ -261,24 +291,11 @@
     for k in FAR_FIRST:
         to = lax.rem(r + k, 16)
         cps.append(push(qs.at[to], q_r.at[k - 1], q_ss.at[k - 1], q_rs.at[k - 1], dp_peer(k)))
-    arrived(3)
-
-    lane = lax.broadcasted_iota(jnp.int32, (R, 2 * R), 1)
-    row = lax.broadcasted_iota(jnp.int32, (R, 2 * R), 0)
-    eye = jnp.where(lane == row + R, 1.0, 0.0)
-    work = jnp.concatenate([gram, jnp.zeros((R, R), F32)], axis=1) + eye
-
-    def eliminate(j, w):
-        rj = jnp.sum(jnp.where(row == j, w, 0.0), axis=0, keepdims=True)
-        cj = jnp.sum(jnp.where(lane == j, w, 0.0), axis=1, keepdims=True)
-        dj = jnp.sum(jnp.where(lane[:1] == j, rj, 0.0), axis=1, keepdims=True)
-        f = jnp.where(row[:, :1] > j, cj / dj, 0.0)
-        return w - f * rj
-
-    work = lax.fori_loop(0, R, eliminate, work)
-    diag = jnp.sum(jnp.where(lane == row, work, 0.0), axis=1, keepdims=True)
-    linv[...] = work[:, R:] / jnp.sqrt(diag)
-
+    g_far("below", below, 2)
+    g_far("above", above, 0)
+    g_far("below", below, 3)
+    arrived_far(0)
+    g_far("above", above, 1)
     for cp in cps:
         cp.wait_recv()
     tot = qf[r]
@@ -287,14 +304,13 @@
     qa[r] = tot.astype(BF)
     cps = [push(qa.at[r], qa.at[r], gq_ss.at[k - 1], gq_rs.at[k - 1], dp_peer(k)) for k in FAR_FIRST]
 
-    g_far("below", below, 3)
-    g_far("above", above, 1)
-    arrived_far(0)
-    for b in range(NB):
-        p_out[BLK * b : BLK * (b + 1), :] = pt[b].T
     g_far("across", across, 0)
     g_far("across", across, 2)
     arrived_far(1)
+    for b in range(NB):
+        p_out[BLK * b : BLK * (b + 1), :] = pt[b].T
+    g_far("across", across, 1)
+    g_far("across", across, 3)
     for cp in cps:
         cp.wait_recv()
 
@@ -311,24 +327,26 @@
         q_out[:, 256 * b : 256 * (b + 1)] = qt
         c_out[:, 256 * b : 256 * (b + 1)] = dot3(linv[...], qt, TN).astype(BF)
 
-    g_far("across", across, 1)
-    g_far("across", across, 3)
     for cp in sent:
         cp.wait_send()
 
 
-def finish_kernel(g0, g1, g2, g3, p_ref, q_ref, c_ref, e_ref, q_out):
-    i = pl.program_id(0)
-    q_out[...] = q_ref[...]
-    at_row = pl.multiple_of(lax.rem(i, 2) * 512, 512)
-    for s, g in enumerate((g0, g1, g2, g3)):
-
-        @pl.when(i // 2 == s)
-        def _(g=g):
-            p = p_ref[pl.ds(pl.multiple_of(i * 512, 512), 512), :]
-            for n in range(7):
-                cols = slice(256 * n, 256 * (n + 1))
-                e_ref[:, cols] = (g[pl.ds(at_row, 512), cols] - dot(p, c_ref[:, cols])).astype(BF)
+def finish_kernel(g0, g1, g2, g3, p_ref, q_ref, c_ref, e_hbm, q_hbm, e_v, sem):
+    q_cp = pltpu.make_async_copy(q_ref, q_hbm, sem.at[0])
+    q_cp.start()
+    cps = [q_cp]
+    for i in range(PIECES):
+        here = slice(D // PIECES * i, D // PIECES * (i + 1))
+        g = (g0, g1, g2, g3)[D // PIECES * i // ROWS]
+        base = D // PIECES * i % ROWS
+        p = p_ref[here, :]
+        for n in range(7):
+            cols = slice(256 * n, 256 * (n + 1))
+            e_v[here, cols] = (g[base : base + D // PIECES, cols] - dot(p, c_ref[:, cols])).astype(BF)
+        cps.append(pltpu.make_async_copy(e_v.at[here], e_hbm.at[here], sem.at[1 + i]))
+        cps[-1].start()
+    for cp in cps:
+        cp.wait()
 
 
 def per_device(activations, output_grads, q_start):
@@ -390,11 +408,11 @@
     )
     new_error, q_factor = pl.pallas_call(
         finish_kernel,
-        grid=(8,),
         out_shape=(jax.ShapeDtypeStruct((D, FFL), BF), jax.ShapeDtypeStruct((R, FFL), F32)),
         in_specs=[vm] * 7,
-        out_specs=(pl.BlockSpec((512, FFL), lambda i: (i, 0)), pl.BlockSpec((R, FFL), lambda i: (0, 0))),
-        compiler_params=pltpu.CompilerParams(vmem_limit_bytes=12 * 2**20),
+        out_specs=(pl.BlockSpec(memory_space=pl.ANY), pl.BlockSpec(memory_space=pl.ANY)),
+        scratch_shapes=[pltpu.VMEM((D, FFL), BF), dma((1 + PIECES,))],
+        compiler_params=pltpu.CompilerParams(vmem_limit_bytes=17 * 2**20),
         name="finish",
     )(*outs)
     return new_error, q_factor.T

time: 68.2 us -> 63.5 us (0.931)
  Pallas kernels: 67.5 us -> 62.6 us
    pallas_call x1, Pallas kernels: 59.1 us -> 56.6 us  [per_device(): pl.pallas_call(factor_kernel, out_shape=[jax.ShapeDtypeStruct((ROWS, FFL)...]
    pallas_call x1, Pallas kernels: 8.31 us -> 6.01 us  [per_device(): pl.pallas_call(finish_kernel, out_shape=(jax.ShapeDtypeStruct((D, FFL), B...]
where the time goes in v3:
time: 63.5 us; the launch traced here: 63.4 us
  Pallas kernels  62.6 us (99%)
  between operations  0.82 us (1%)
    pallas_call x1, Pallas kernels, per_device(): pl.pallas_call(factor_kernel, out_shape=[jax.ShapeDtypeStruct((ROWS, FFL)...  56.6 us
    pallas_call x1, Pallas kernels, per_device(): pl.pallas_call(finish_kernel, out_shape=(jax.ShapeDtypeStruct((D, FFL), B...  6.01 us

profile of v3, /device:TPU:1, one launch (start us, length us, event | category | flops | bytes accessed | tf_op | source)
XLA Modules:
  0.0 63.4 jit_solution(8095030677162022282)
XLA Ops:
  0.6 56.6 %factors.1 = (f32[1024,1792]{1,0:T(8,128)S(1)}, f32[1024,1792]{1,0:T(8,128)S(1)}, f32[1024,1792]{1,0:T(8,128)S(1)}, f32[1024,1792]{1,0:T(8,128)S(1)}, bf16[4096,...) custom-call(bf16[128,4096]{1,0:T(8,128)(2,1)} %x_hbm.1, bf16[1024,1792]{1,0:T(8,128)(2,1)} %y_hbm.1, ...), custom_call_target="tpu_custom_call" | custom-call | tf_op jit(solution)/shard_map/factors/pallas_call | solution.py:355
  57.2 6.0 %finish.1 = (bf16[4096,1792]{1,0:T(8,128)(2,1)}, f32[64,1792]{1,0:T(8,128)}) custom-call(f32[1024,1792]{1,0:T(8,128)S(1)} %get-tuple-element.11.g0, f32[1024,1792]{1,0:T(8,128)S(1)} %get-tuple-element.12.g1, f32[1024,1792]{1,0:T(8,128)S(1)} %get-tuple-element.13.g2, f32[1024,1792]{1,0:T(8,128)S(1)} %get-tuple-element.14.g3, ...), custom_call_target="tpu_custom_call" | custom-call | tf_op jit(solution)/shard_map/finish/pallas_call | solution.py:409
